TPU v7x, 32 devices: a whole 2x2x4 slice. The times are simulated.
32 devices in a mesh: gx: 4 (over y, core), gy: 2 (over x), gz: 4 (over z).
Axes of the slice: x: 2, y: 2, z: 4, core: 2. Of those that a mesh axis runs over, the one named last changes fastest.
Arguments:
- pressure_now: float32 [64, 64, 512], P('gx', 'gy', 'gz'), may hold values from -6 to 6
- pressure_before: float32 [64, 64, 512], P('gx', 'gy', 'gz'), may hold values from -6 to 6
- region_code: int32 [64, 64, 512], P('gx', 'gy', 'gz'), may hold values from 0 to 7
- velocity: float32 [8], replicated, may hold values from 0.2 to 0.42
- wavelet: float32 [6, 16], replicated, may hold values from -6 to 6
- source_cell: int32 [16], replicated, may hold values from 0 to 2097151
Outputs:
- pressure: float32 [64, 64, 512], P('gx', 'gy', 'gz')
- previous: float32 [64, 64, 512], P('gx', 'gy', 'gz')
Inputs may be any that keep to these rules, and one draw needn't show every extreme that they name: source_cell[s] is the flat index x * 64 * 512 + y * 512 + z of a grid cell; sources may share a cell.
All inputs are finite; a program needn't handle non-finite values.
Results may differ from a plain program's by a relative error of at most 0.00002.
Values sent between devices are 32-bit elements; how exact they have to be, the bound alone decides.
A program may use at most 64 MiB of HBM per device.

v0:
```python
import functools

import jax
import jax.numpy as jnp
from jax import lax
from jax.experimental import pallas as pl
from jax.experimental.pallas import tpu as pltpu
from jax.sharding import PartitionSpec as P

STEPS = 6
CENTRE = -205.0 / 72.0
C1, C2, C3, C4 = (8.0 / 5.0, -1.0 / 5.0, 8.0 / 315.0, -1.0 / 560.0)
WEIGHTS = (C1, C2, C3, C4)
W = 4
CHUNKS = 1
T = 8
LANES = 128
MESH = pl.DeviceIdType.MESH
def kernel(sizes, now_hbm, before_hbm, code_hbm, vel_ref, wave_ref, src_ref, out_ref, prev_ref,
           field0, field1, state0, state1, pack0, pack1, halo, rate, code, source, edge, send_sem, recv_sem, load_sem):
    field, state, pack = (field0, field1), (state0, state1), (pack0, pack1)
    (nx, ny, nz), (gx, gy, gz) = sizes
    grid_y, grid_z = ny * gy, nz * gz
    lanes_of = ny // 8
    slabs = LANES // 8 // lanes_of
    packs = nx // slabs
    ix, iy, iz = lax.axis_index("gx"), lax.axis_index("gy"), lax.axis_index("gz")
    targets = (
        (({"gx": lax.rem(ix + gx - 1, gx)}, None), ({"gx": lax.rem(ix + 1, gx)}, None)),
        (({"gy": iy - 1}, iy > 0), ({"gy": iy + 1}, iy < gy - 1)),
        (({"gz": iz - 1}, iz > 0), ({"gz": iz + 1}, iz < gz - 1)),
    )

    def guarded(condition, action):
        if condition is None:
            action()
        else:
            pl.when(condition)(action)

    own_x, own_y = pl.ds(0, nx), pl.ds(T, ny)
    half = lanes_of // CHUNKS
    loads = [
        pltpu.make_async_copy(now_hbm, field[0].at[own_x, own_y], load_sem.at[0]),
        pltpu.make_async_copy(before_hbm, field[1].at[own_x, own_y], load_sem.at[1]),
        pltpu.make_async_copy(code_hbm, code, load_sem.at[2]),
    ]
    for load in loads:
        load.start()

    nothing = jnp.zeros((nx, T, LANES), jnp.float32)
    for par in range(2):
        field[par][own_x, 0:T, :] = nothing
        field[par][own_x, pl.ds(T + ny, T), :] = nothing
    edge[...] = jnp.zeros_like(edge)

    barrier = pltpu.get_barrier_semaphore()
    for sides in targets:
        for target, present in sides:
            guarded(present, lambda target=target: pl.semaphore_signal(
                barrier, inc=1, device_id=target, device_id_type=MESH))

    inner = packs - 2

    def group(name, par):
        pieces = []
        if name[0] == "x":
            base = 2 * name[1]
            part = pl.ds(name[1] * half, half)
            pieces = [(0, state[par].at[pl.ds(0, W), part], halo.at[par, 1, name[1]]),
                      (0, state[par].at[pl.ds(nx - W, W), part], halo.at[par, 0, name[1]])]
        else:
            axis = 1 if name[0] == "y" else 2
            base = 2 * CHUNKS + (0 if axis == 1 else 6)
            if axis == 1:
                low, high = pl.ds(T, T), pl.ds(ny, T)
                over, under = pl.ds(T + ny, T), pl.ds(0, T)
                if name[1] == "face":
                    spans = [pl.ds(0, slabs), pl.ds(nx - slabs, slabs)]
                else:
                    spans = [pl.ds(slabs, nx - 2 * slabs)]
                    base = base + 4
                for span in spans:
                    pieces.append((1, field[par].at[span, low], field[par].at[span, over]))
                    pieces.append((1, field[par].at[span, high], field[par].at[span, under]))
            else:
                span = pl.ds(0, 2) if name[1] == "face" else pl.ds(2, inner)
                base = base + (0 if name[1] == "face" else 2)
                pieces.append((2, pack[par].at[span], edge.at[par, 1, span]))
                pieces.append((2, pack[par].at[span], edge.at[par, 0, span]))
        result = []
        for n, (axis, src, dst) in enumerate(pieces):
            target, present = targets[axis][n % 2]
            copy = pltpu.make_async_remote_copy(
                src_ref=src, dst_ref=dst, send_sem=send_sem.at[par, base + n], recv_sem=recv_sem.at[par, base + n],
                device_id=target, device_id_type=MESH)
            result.append((copy, present, targets[axis][1 - n % 2][1]))
        return result

    def start(name, par):
        for copy, to_here, _ in group(name, par):
            guarded(to_here, copy.start)

    def wait_send(name, par):
        for copy, to_here, _ in group(name, par):
            guarded(to_here, copy.wait_send)

    def wait_recv(name, par):
        for copy, _, from_here in group(name, par):
            guarded(from_here, copy.wait_recv)

    chunks = [("x", n) for n in range(CHUNKS)]
    every = chunks + [("y", "face"), ("z", "face"), ("y", "inner"), ("z", "inner")]

    lane = lax.broadcasted_iota(jnp.int32, (8, LANES), 1)
    group_of, place = lane // 8, lane % 8

    def packed(value, g, total):
        return jnp.where(group_of == g, pltpu.roll(value, (W + 8 * g) % LANES, 1), total)

    def rows(j):
        return pl.ds(T + j, 8, stride=lanes_of)

    zero = jnp.zeros((8, LANES), jnp.float32)
    ends = ((0, 0, 0), (1, 1, nx - slabs))

    loads[0].wait()
    for side, slot, first in ends:
        total = zero
        for a in range(slabs):
            for j in range(lanes_of):
                value = field[0][first + a, rows(j), :]
                state[0][first + a, j] = value
                total = packed(value, a * lanes_of + j, total)
        pack[0][slot] = total
    peers = 2
    for sides in targets[1:]:
        for _, present in sides:
            peers = peers + present.astype(jnp.int32)
    pl.semaphore_wait(barrier, peers)
    for name in chunks + [("y", "face"), ("z", "face"), ("y", "inner")]:
        start(name, 0)

    def first_pack(m, carry):
        total = zero
        for a in range(slabs):
            for j in range(lanes_of):
                value = field[0][m * slabs + slabs + a, rows(j), :]
                state[0][m * slabs + slabs + a, j] = value
                total = packed(value, a * lanes_of + j, total)
        pack[0][2 + m] = total
        return carry

    lax.fori_loop(0, inner, first_pack, 0)
    start(("z", "inner"), 0)

    loads[2].wait()
    squares = [vel_ref[n] * vel_ref[n] for n in range(vel_ref.shape[0])]

    def rate_slab(x, carry):
        for j in range(lanes_of):
            codes = code[x, pl.ds(j, 8, stride=lanes_of), :]
            value = jnp.full(codes.shape, squares[0], jnp.float32)
            for n in range(1, len(squares)):
                value = jnp.where(codes == n, squares[n], value)
            rate[x, j] = value
        return carry

    lax.fori_loop(0, nx, rate_slab, 0)

    count = src_ref.shape[0]
    row_at = jnp.full((1, LANES), -1, jnp.int32)
    lane_row = lax.broadcasted_iota(jnp.int32, (1, LANES), 1)
    slot_col = lax.broadcasted_iota(jnp.int32, (LANES, LANES), 0)
    z_at = jnp.full((LANES, LANES), -1, jnp.int32)
    for s in range(count):
        cell = src_ref[s]
        sx = cell // (grid_y * grid_z) - ix * nx
        sy = cell // grid_z % grid_y - iy * ny
        sz = cell % grid_z - iz * nz
        here = (sx >= 0) & (sx < nx) & (sy >= 0) & (sy < ny)
        local = jnp.where(here, sx * ny + sy % lanes_of * 8 + sy // lanes_of, -1)
        row_at = jnp.where((lane_row % count == s) & (lane_row < 3 * count), local, row_at)
        z_at = jnp.where((slot_col % count == s) & (slot_col < 3 * count), sz, z_at)
    spread = (z_at == lax.broadcasted_iota(jnp.int32, (LANES, LANES), 1)).astype(jnp.float32).astype(jnp.bfloat16)

    def source_field(t):
        wave = jnp.zeros((1, LANES), jnp.float32)
        for s in range(count):
            wave = jnp.where(lane_row % count == s, wave_ref[t, s], wave)
        high = wave.astype(jnp.bfloat16).astype(jnp.float32)
        rest = wave - high
        middle = rest.astype(jnp.bfloat16).astype(jnp.float32)
        parts = jnp.where(lane_row < count, high, jnp.where(lane_row < 2 * count, middle, rest - middle))
        block = slabs * ny

        def chunk(m, carry):
            row = lax.broadcasted_iota(jnp.int32, (block, LANES), 0) + m * block
            picks = jnp.where(row == row_at, parts, 0.0).astype(jnp.bfloat16)
            value = jnp.dot(picks, spread, preferred_element_type=jnp.float32)
            source[pl.ds(m * slabs, slabs)] = value.reshape(slabs, lanes_of, 8, LANES)
            return carry

        lax.fori_loop(0, packs, chunk, 0)

    near_edge = (lane < W) | (lane >= LANES - W)
    take_up = [jnp.where((place >= W) & (place - k < W), WEIGHTS[k - 1], 0.0) for k in range(1, W + 1)]
    take_down = [jnp.where((place < W) & (place + k >= W), WEIGHTS[k - 1], 0.0) for k in range(1, W + 1)]

    def edge_fix(cur, slot):
        delta = jnp.where(place < W, edge[cur, 0, slot], edge[cur, 1, slot]) - pack[cur][slot]
        fix = zero
        for k in range(1, W + 1):
            fix = fix + take_up[k - 1] * pltpu.roll(delta, k, 1)
            fix = fix + take_down[k - 1] * pltpu.roll(delta, LANES - k, 1)
        return fix

    def cell_rows(cur, nxt, x, a, js, fix, layer):
        shifted = {}
        for o in range(js[0] - W, js[-1] + W + 1):
            if 0 <= o < lanes_of:
                shifted[o] = state[cur][x, o]
            else:
                shifted[o] = field[cur][x, pl.ds(T + o, 8, stride=lanes_of), :]
        values = []
        for j in js:
            f = shifted[j]
            acc = (3.0 * CENTRE) * f
            for k in range(1, W + 1):
                acc = acc + WEIGHTS[k - 1] * ((layer(k, j) + layer(-k, j)) + (shifted[j + k] + shifted[j - k]))
            below, above = pltpu.roll(f, 1, 1), pltpu.roll(f, LANES - 1, 1)
            far_below = C4 * below + C3 * f + C2 * above
            far_above = C2 * below + C3 * f + C4 * above
            acc = acc + C1 * (below + above)
            acc = acc + pltpu.roll(far_below, 3, 1) + pltpu.roll(far_above, LANES - 3, 1)
            back = (2 * LANES - W - 8 * (a * lanes_of + j)) % LANES
            acc = acc + jnp.where(near_edge, pltpu.roll(fix, back, 1), 0.0)
            values.append((2.0 * f - state[nxt][x, j]) + rate[x, j] * acc + source[x, j])
        return values

    def first_before(x, carry):
        for j in range(lanes_of):
            state[1][x, j] = field[1][x, rows(j), :]
        return carry

    loads[1].wait()
    lax.fori_loop(0, nx, first_before, 0)
    for t in range(STEPS):
        cur, nxt = t % 2, (t + 1) % 2
        last = t == STEPS - 1

        def put(x, j, value):
            own = pl.ds(j, 8, stride=lanes_of)
            if last:
                out_ref[x, own, :] = value
            else:
                state[nxt][x, j] = value
                field[nxt][x, rows(j), :] = value
            if t == STEPS - 2:
                prev_ref[x, own, :] = value

        source_field(t)
        if t >= 1:
            for name in every:
                wait_send(name, nxt)
        wait_recv(("z", "face"), cur)
        wait_recv(("y", "face"), cur)
        fixes = [edge_fix(cur, slot) for _, slot, _ in ends]
        totals = [zero, zero]
        for n in range(CHUNKS):
            wait_recv(("x", n), cur)
            js = range(n * half, n * half + half)
            for side, slot, first in ends:
                for a in range(slabs):
                    x = first + a

                    def layer(k, j, x=x, n=n):
                        if x + k < 0:
                            return halo[cur, 0, n, x + k + W, j - n * half]
                        if x + k >= nx:
                            return halo[cur, 1, n, x + k - nx, j - n * half]
                        return state[cur][x + k, j]

                    for j, value in zip(js, cell_rows(cur, nxt, x, a, js, fixes[slot], layer)):
                        put(x, j, value)
                        if not last:
                            totals[slot] = packed(value, a * lanes_of + j, totals[slot])
            if not last:
                start(("x", n), nxt)
        if not last:
            for _, slot, _ in ends:
                pack[nxt][slot] = totals[slot]
            start(("z", "face"), nxt)
            start(("y", "face"), nxt)
        wait_recv(("z", "inner"), cur)
        wait_recv(("y", "inner"), cur)

        def block(m, carry):
            fix = edge_fix(cur, 2 + m)
            total = zero
            for a in range(slabs):
                x = m * slabs + slabs + a
                js = range(lanes_of)
                near = lambda k, j: state[cur][x + k, j]
                for j, value in zip(js, cell_rows(cur, nxt, x, a, js, fix, near)):
                    put(x, j, value)
                    if not last:
                        total = packed(value, a * lanes_of + j, total)
            if not last:
                pack[nxt][2 + m] = total
            return carry

        lax.fori_loop(0, inner, block, 0)
        if not last:
            start(("z", "inner"), nxt)
            start(("y", "inner"), nxt)
    for name in every:
        wait_send(name, (STEPS - 1) % 2)


def move_out(first_ref, second_ref, first_out, second_out, sem):
    moves = [
        pltpu.make_async_copy(first_ref, first_out, sem.at[0]),
        pltpu.make_async_copy(second_ref, second_out, sem.at[1]),
    ]
    for move in moves:
        move.start()
    for move in moves:
        move.wait()


def solution(mesh):
    counts = tuple(mesh.shape[name] for name in ("gx", "gy", "gz"))

    def per_device(now, before, codes, velocity, wavelet, source_cell):
        nx, ny, nz = now.shape
        anywhere = pl.BlockSpec(memory_space=pl.ANY)
        scalars = pl.BlockSpec(memory_space=pltpu.SMEM)
        packs = nx * ny // LANES
        copies = 2 * CHUNKS + 10
        results = pl.pallas_call(
            functools.partial(kernel, (now.shape, counts)),
            out_shape=(pltpu.VMEM(now.shape, jnp.float32),) * 2,
            in_specs=[anywhere] * 3 + [scalars] * 3,
            out_specs=(pl.BlockSpec(memory_space=pltpu.VMEM),) * 2,
            scratch_shapes=[
                pltpu.VMEM((nx, ny + 2 * T, nz), jnp.float32),
                pltpu.VMEM((nx, ny + 2 * T, nz), jnp.float32),
                pltpu.VMEM((nx, ny // 8, 8, nz), jnp.float32),
                pltpu.VMEM((nx, ny // 8, 8, nz), jnp.float32),
                pltpu.VMEM((packs, 8, LANES), jnp.float32),
                pltpu.VMEM((packs, 8, LANES), jnp.float32),
                pltpu.VMEM((2, 2, CHUNKS, W, ny // 8 // CHUNKS, 8, nz), jnp.float32),
                pltpu.VMEM((nx, ny // 8, 8, nz), jnp.float32),
                pltpu.VMEM((nx, ny, nz), jnp.int32),
                pltpu.VMEM((nx, ny // 8, 8, nz), jnp.float32),
                pltpu.VMEM((2, 2, packs, 8, LANES), jnp.float32),
                pltpu.SemaphoreType.DMA((2, copies)),
                pltpu.SemaphoreType.DMA((2, copies)),
                pltpu.SemaphoreType.DMA((3,)),
            ],
            compiler_params=pltpu.CompilerParams(collective_id=0, has_side_effects=True),
        )(now, before, codes, velocity, wavelet, source_cell)
        return pl.pallas_call(
            move_out,
            out_shape=(jax.ShapeDtypeStruct(now.shape, jnp.float32),) * 2,
            in_specs=[pl.BlockSpec(memory_space=pltpu.VMEM)] * 2,
            out_specs=(anywhere, anywhere),
            scratch_shapes=[pltpu.SemaphoreType.DMA((2,))],
            compiler_params=pltpu.CompilerParams(vmem_limit_bytes=2**20),
        )(*[pltpu.with_memory_space_constraint(value, pltpu.VMEM) for value in results])

    block = P("gx", "gy", "gz")
    return jax.shard_map(
        per_device,
        mesh=mesh,
        in_specs=(block, block, block, P(), P(), P()),
        out_specs=(block, block),
        check_vma=False,
    )
```

profile of v0, /device:TPU:0, one launch (start us, length us, event | category | flops | bytes accessed | tf_op | source)
XLA Modules:
  0.0 28.7 jit_solution(14627282900959597855)
XLA Ops:
  0.6 27.2 %shard_map.77 = (f32[16,32,128]{2,1,0:T(8,128)S(1)}, f32[16,32,128]{2,1,0:T(8,128)S(1)}) custom-call(f32[16,32,128]{2,1,0:T(8,128)} %now_hbm.1, f32[16,32,128]{2,1,0:T(8,128)} %before_hbm.1, s32[16,32,128]{2,1,0:T(8,128)} %code_hbm.1, f32[8]{0:T(128)} %vel_ref.1, f32[6,16]{1,0:T(8,128)} %wave_ref.1, s32[16]{0:T(128)} %src_ref.1), custom_call_target="tpu_custom_call" | custom-call | tf_op jit(solution)/shard_map/pallas_call | solution.py:340
  27.9 0.8 %shard_map.78 = (f32[16,32,128]{2,1,0:T(8,128)}, f32[16,32,128]{2,1,0:T(8,128)}) custom-call(f32[16,32,128]{2,1,0:T(8,128)S(1)} %get-tuple-element.4.first_ref, f32[16,32,128]{2,1,0:T(8,128)S(1)} %get-tuple-element.5.second_ref), custom_call_target="tpu_custom_call" | custom-call | tf_op jit(solution)/shard_map/pallas_call | solution.py:363
where the time goes:
time: 28.9 us; the launch traced here: 28.7 us
  Pallas kernels  28 us (97%)
  between operations  0.64 us (2%)
    pallas_call x1, Pallas kernels, per_device(): pl.pallas_call(functools.partial(kernel, (now.shape, counts)), out_shape=...  27.2 us
    pallas_call x1, Pallas kernels, per_device(): pl.pallas_call(move_out, out_shape=(jax.ShapeDtypeStruct(now.shape, jnp.f...  0.81 us

commit v1 on v0

--- a/solution.py
+++ b/solution.py
@@ -10,15 +10,17 @@
 STEPS = 6
 CENTRE = -205.0 / 72.0
 C1, C2, C3, C4 = (8.0 / 5.0, -1.0 / 5.0, 8.0 / 315.0, -1.0 / 560.0)
-WEIGHTS = (C1, C2, C3, C4)
+SCALE = 5040.0
+WEIGHTS = tuple(round(SCALE * c) * 1.0 for c in (C1, C2, C3, C4))
 W = 4
 CHUNKS = 1
 T = 8
 LANES = 128
 MESH = pl.DeviceIdType.MESH
 def kernel(sizes, now_hbm, before_hbm, code_hbm, vel_ref, wave_ref, src_ref, out_ref, prev_ref,
-           field0, field1, state0, state1, pack0, pack1, halo, rate, code, source, edge, send_sem, recv_sem, load_sem):
-    field, state, pack = (field0, field1), (state0, state1), (pack0, pack1)
+           field0, field1, beside0, beside1, state0, state1, pack0, pack1, halo, rate, coef, code, source, edge,
+           along, along_z, from_edge, only, send_sem, recv_sem, load_sem):
+    field, beside, state, pack = (field0, field1), (beside0, beside1), (state0, state1), (pack0, pack1)
     (nx, ny, nz), (gx, gy, gz) = sizes
     grid_y, grid_z = ny * gy, nz * gz
     lanes_of = ny // 8
@@ -51,6 +53,7 @@
     for par in range(2):
         field[par][own_x, 0:T, :] = nothing
         field[par][own_x, pl.ds(T + ny, T), :] = nothing
+        beside[par][...] = jnp.zeros_like(beside[par])
     edge[...] = jnp.zeros_like(edge)
 
     barrier = pltpu.get_barrier_semaphore()
@@ -72,16 +75,16 @@
             axis = 1 if name[0] == "y" else 2
             base = 2 * CHUNKS + (0 if axis == 1 else 6)
             if axis == 1:
-                low, high = pl.ds(T, T), pl.ds(ny, T)
-                over, under = pl.ds(T + ny, T), pl.ds(0, T)
+                low, high = pl.ds(T, W), pl.ds(T + ny - W, W)
+                over, under = pl.ds(T + ny, W), pl.ds(T - W, W)
                 if name[1] == "face":
                     spans = [pl.ds(0, slabs), pl.ds(nx - slabs, slabs)]
                 else:
                     spans = [pl.ds(slabs, nx - 2 * slabs)]
                     base = base + 4
                 for span in spans:
-                    pieces.append((1, field[par].at[span, low], field[par].at[span, over]))
-                    pieces.append((1, field[par].at[span, high], field[par].at[span, under]))
+                    pieces.append((1, field[par].at[span, low], beside[par].at[span, over]))
+                    pieces.append((1, field[par].at[span, high], beside[par].at[span, under]))
             else:
                 span = pl.ds(0, 2) if name[1] == "face" else pl.ds(2, inner)
                 base = base + (0 if name[1] == "face" else 2)
@@ -162,7 +165,8 @@
             value = jnp.full(codes.shape, squares[0], jnp.float32)
             for n in range(1, len(squares)):
                 value = jnp.where(codes == n, squares[n], value)
-            rate[x, j] = value
+            rate[x, j] = value * (1.0 / SCALE)
+            coef[x, j] = 2.0 + (3.0 * CENTRE) * value
         return carry
 
     lax.fori_loop(0, nx, rate_slab, 0)
@@ -202,40 +206,90 @@
 
         lax.fori_loop(0, packs, chunk, 0)
 
-    near_edge = (lane < W) | (lane >= LANES - W)
-    take_up = [jnp.where((place >= W) & (place - k < W), WEIGHTS[k - 1], 0.0) for k in range(1, W + 1)]
-    take_down = [jnp.where((place < W) & (place + k >= W), WEIGHTS[k - 1], 0.0) for k in range(1, W + 1)]
-
-    def edge_fix(cur, slot):
-        delta = jnp.where(place < W, edge[cur, 0, slot], edge[cur, 1, slot]) - pack[cur][slot]
-        fix = zero
+    row_in = lax.broadcasted_iota(jnp.int32, (LANES, LANES), 0)
+    col_in = lax.broadcasted_iota(jnp.int32, (LANES, LANES), 1)
+    spot = row_in % 8
+    halo_at = jnp.where(spot < W, spot - W, LANES + spot - W)
+
+    def taps(distance):
+        value = jnp.zeros((LANES, LANES), jnp.float32)
         for k in range(1, W + 1):
-            fix = fix + take_up[k - 1] * pltpu.roll(delta, k, 1)
-            fix = fix + take_down[k - 1] * pltpu.roll(delta, LANES - k, 1)
-        return fix
-
-    def cell_rows(cur, nxt, x, a, js, fix, layer):
-        shifted = {}
-        for o in range(js[0] - W, js[-1] + W + 1):
-            if 0 <= o < lanes_of:
-                shifted[o] = state[cur][x, o]
+            value = jnp.where((distance == k) | (distance == -k), WEIGHTS[k - 1], value)
+        return value.astype(jnp.bfloat16)
+
+    for part in range(2):
+        along_z[pl.ds(part * LANES, LANES), :] = taps(row_in - col_in)
+        from_edge[pl.ds(part * LANES, LANES), :] = taps(halo_at - col_in)
+    double_lane = lax.broadcasted_iota(jnp.int32, (16, LANES), 1) // 8
+    double_row = lax.broadcasted_iota(jnp.int32, (16, LANES), 0) // 8
+    for pair in range(8):
+        only[pair] = (double_lane == 2 * pair + double_row).astype(jnp.float32).astype(jnp.bfloat16)
+
+    def split(value):
+        high = value.astype(jnp.bfloat16)
+        return high, (value - high.astype(jnp.float32)).astype(jnp.bfloat16)
+
+    def z_own(cur):
+        value = state[cur][...].reshape(nx * ny, LANES)
+        total = jnp.dot(jnp.concatenate(split(value), axis=1), along_z[...], preferred_element_type=jnp.float32)
+        along[...] = total.reshape(nx, lanes_of, 8, LANES)
+
+    def z_beside(cur, slots):
+        picked = []
+        for slot in slots:
+            value = jnp.where(place < W, edge[cur, 0, slot], edge[cur, 1, slot])
+            high, low = split(jnp.concatenate([value, value], axis=0))
+            picked += [jnp.concatenate([high * only[pair], low * only[pair]], axis=1) for pair in range(8)]
+        total = jnp.dot(jnp.concatenate(picked, axis=0), from_edge[...], preferred_element_type=jnp.float32)
+        return total.reshape(len(slots), slabs, lanes_of, 8, LANES)
+
+    def own_part(cur, nxt, first, ends):
+        for a in range(slabs):
+            x = first + a
+            shifted = {}
+            for o in range(-W, lanes_of + W):
+                if 0 <= o < lanes_of:
+                    shifted[o] = state[cur][x, o]
+                else:
+                    shifted[o] = field[cur][x, pl.ds(T + o, 8, stride=lanes_of), :]
+            for j in range(lanes_of):
+                acc = along[x, j]
+                for k in range(1, W + 1):
+                    near = shifted[j + k] + shifted[j - k]
+                    if not ends or x + k < nx:
+                        near = near + state[cur][x + k, j]
+                    if not ends or x - k >= 0:
+                        near = near + state[cur][x - k, j]
+                    acc = acc + WEIGHTS[k - 1] * near
+                state[nxt][x, j] = (coef[x, j] * shifted[j] - state[nxt][x, j]) + (rate[x, j] * acc + source[x, j])
+
+    def yz_part(cur, nxt, first, beyond):
+        results = {}
+        for a in range(slabs):
+            x = first + a
+            outer = {o: beside[cur][x, pl.ds(T + o, 8, stride=lanes_of), :]
+                     for o in list(range(-W, 0)) + list(range(lanes_of, lanes_of + W))}
+            for j in range(lanes_of):
+                acc = beyond[a, j]
+                for k in range(1, W + 1):
+                    if j - k < 0:
+                        acc = acc + WEIGHTS[k - 1] * outer[j - k]
+                    if j + k >= lanes_of:
+                        acc = acc + WEIGHTS[k - 1] * outer[j + k]
+                results[a, j] = state[nxt][x, j] + rate[x, j] * acc
+        return results
+
+    def x_part(cur, nxt, x, j, n):
+        acc = None
+        for k in range(1, W + 1):
+            if x - k < 0:
+                term = WEIGHTS[k - 1] * halo[cur, 0, n, x - k + W, j - n * half]
+            elif x + k >= nx:
+                term = WEIGHTS[k - 1] * halo[cur, 1, n, x + k - nx, j - n * half]
             else:
-                shifted[o] = field[cur][x, pl.ds(T + o, 8, stride=lanes_of), :]
-        values = []
-        for j in js:
-            f = shifted[j]
-            acc = (3.0 * CENTRE) * f
-            for k in range(1, W + 1):
-                acc = acc + WEIGHTS[k - 1] * ((layer(k, j) + layer(-k, j)) + (shifted[j + k] + shifted[j - k]))
-            below, above = pltpu.roll(f, 1, 1), pltpu.roll(f, LANES - 1, 1)
-            far_below = C4 * below + C3 * f + C2 * above
-            far_above = C2 * below + C3 * f + C4 * above
-            acc = acc + C1 * (below + above)
-            acc = acc + pltpu.roll(far_below, 3, 1) + pltpu.roll(far_above, LANES - 3, 1)
-            back = (2 * LANES - W - 8 * (a * lanes_of + j)) % LANES
-            acc = acc + jnp.where(near_edge, pltpu.roll(fix, back, 1), 0.0)
-            values.append((2.0 * f - state[nxt][x, j]) + rate[x, j] * acc + source[x, j])
-        return values
+                continue
+            acc = term if acc is None else acc + term
+        return state[nxt][x, j] + rate[x, j] * acc
 
     def first_before(x, carry):
         for j in range(lanes_of):
@@ -262,54 +316,48 @@
         if t >= 1:
             for name in every:
                 wait_send(name, nxt)
+        z_own(cur)
+        for _, _, first in ends:
+            own_part(cur, nxt, first, True)
+        for m in range(inner):
+            own_part(cur, nxt, m * slabs + slabs, False)
         wait_recv(("z", "face"), cur)
         wait_recv(("y", "face"), cur)
-        fixes = [edge_fix(cur, slot) for _, slot, _ in ends]
+        beyond = z_beside(cur, [slot for _, slot, _ in ends])
+        for n, (_, slot, first) in enumerate(ends):
+            for (a, j), value in yz_part(cur, nxt, first, beyond[n]).items():
+                state[nxt][first + a, j] = value
         totals = [zero, zero]
         for n in range(CHUNKS):
             wait_recv(("x", n), cur)
             js = range(n * half, n * half + half)
             for side, slot, first in ends:
                 for a in range(slabs):
-                    x = first + a
-
-                    def layer(k, j, x=x, n=n):
-                        if x + k < 0:
-                            return halo[cur, 0, n, x + k + W, j - n * half]
-                        if x + k >= nx:
-                            return halo[cur, 1, n, x + k - nx, j - n * half]
-                        return state[cur][x + k, j]
-
-                    for j, value in zip(js, cell_rows(cur, nxt, x, a, js, fixes[slot], layer)):
-                        put(x, j, value)
+                    for j in js:
+                        value = x_part(cur, nxt, first + a, j, n)
+                        put(first + a, j, value)
                         if not last:
                             totals[slot] = packed(value, a * lanes_of + j, totals[slot])
             if not last:
                 start(("x", n), nxt)
         if not last:
+            start(("y", "face"), nxt)
             for _, slot, _ in ends:
                 pack[nxt][slot] = totals[slot]
             start(("z", "face"), nxt)
-            start(("y", "face"), nxt)
         wait_recv(("z", "inner"), cur)
         wait_recv(("y", "inner"), cur)
 
-        def block(m, carry):
-            fix = edge_fix(cur, 2 + m)
+        beyond = z_beside(cur, range(2, packs))
+        for m in range(inner):
             total = zero
-            for a in range(slabs):
-                x = m * slabs + slabs + a
-                js = range(lanes_of)
-                near = lambda k, j: state[cur][x + k, j]
-                for j, value in zip(js, cell_rows(cur, nxt, x, a, js, fix, near)):
-                    put(x, j, value)
-                    if not last:
-                        total = packed(value, a * lanes_of + j, total)
+            first = m * slabs + slabs
+            for (a, j), value in yz_part(cur, nxt, first, beyond[m]).items():
+                put(first + a, j, value)
+                if not last:
+                    total = packed(value, a * lanes_of + j, total)
             if not last:
                 pack[nxt][2 + m] = total
-            return carry
-
-        lax.fori_loop(0, inner, block, 0)
         if not last:
             start(("z", "inner"), nxt)
             start(("y", "inner"), nxt)
@@ -345,15 +393,22 @@
             scratch_shapes=[
                 pltpu.VMEM((nx, ny + 2 * T, nz), jnp.float32),
                 pltpu.VMEM((nx, ny + 2 * T, nz), jnp.float32),
+                pltpu.VMEM((nx, ny + 2 * T, nz), jnp.float32),
+                pltpu.VMEM((nx, ny + 2 * T, nz), jnp.float32),
                 pltpu.VMEM((nx, ny // 8, 8, nz), jnp.float32),
                 pltpu.VMEM((nx, ny // 8, 8, nz), jnp.float32),
                 pltpu.VMEM((packs, 8, LANES), jnp.float32),
                 pltpu.VMEM((packs, 8, LANES), jnp.float32),
                 pltpu.VMEM((2, 2, CHUNKS, W, ny // 8 // CHUNKS, 8, nz), jnp.float32),
                 pltpu.VMEM((nx, ny // 8, 8, nz), jnp.float32),
+                pltpu.VMEM((nx, ny // 8, 8, nz), jnp.float32),
                 pltpu.VMEM((nx, ny, nz), jnp.int32),
                 pltpu.VMEM((nx, ny // 8, 8, nz), jnp.float32),
                 pltpu.VMEM((2, 2, packs, 8, LANES), jnp.float32),
+                pltpu.VMEM((nx, ny // 8, 8, nz), jnp.float32),
+                pltpu.VMEM((2 * LANES, LANES), jnp.bfloat16),
+                pltpu.VMEM((2 * LANES, LANES), jnp.bfloat16),
+                pltpu.VMEM((8, 16, LANES), jnp.bfloat16),
                 pltpu.SemaphoreType.DMA((2, copies)),
                 pltpu.SemaphoreType.DMA((2, copies)),
                 pltpu.SemaphoreType.DMA((3,)),

time: 28.9 us -> 26.8 us (0.927)
  Pallas kernels: 28 us -> 25.9 us
    pallas_call x1, Pallas kernels: 27.2 us -> 25.1 us  [per_device(): pl.pallas_call(functools.partial(kernel, (now.shape, counts)), out_shape=...]
where the time goes in v1:
time: 26.8 us; the launch traced here: 26.6 us
  Pallas kernels  25.9 us (97%)
  between operations  0.64 us (2%)
    pallas_call x1, Pallas kernels, per_device(): pl.pallas_call(functools.partial(kernel, (now.shape, counts)), out_shape=...  25.1 us
    pallas_call x1, Pallas kernels, per_device(): pl.pallas_call(move_out, out_shape=(jax.ShapeDtypeStruct(now.shape, jnp.f...  0.81 us

profile of v1, /device:TPU:0, one launch (start us, length us, event | category | flops | bytes accessed | tf_op | source)
XLA Modules:
  0.0 26.6 jit_solution(9809686679759924500)
XLA Ops:
  0.6 25.1 %shard_map.77 = (f32[16,32,128]{2,1,0:T(8,128)S(1)}, f32[16,32,128]{2,1,0:T(8,128)S(1)}) custom-call(f32[16,32,128]{2,1,0:T(8,128)} %now_hbm.1, f32[16,32,128]{2,1,0:T(8,128)} %before_hbm.1, s32[16,32,128]{2,1,0:T(8,128)} %code_hbm.1, f32[8]{0:T(128)} %vel_ref.1, f32[6,16]{1,0:T(8,128)} %wave_ref.1, s32[16]{0:T(128)} %src_ref.1), custom_call_target="tpu_custom_call" | custom-call | tf_op jit(solution)/shard_map/pallas_call | solution.py:388
  25.8 0.8 %shard_map.78 = (f32[16,32,128]{2,1,0:T(8,128)}, f32[16,32,128]{2,1,0:T(8,128)}) custom-call(f32[16,32,128]{2,1,0:T(8,128)S(1)} %get-tuple-element.4.first_ref, f32[16,32,128]{2,1,0:T(8,128)S(1)} %get-tuple-element.5.second_ref), custom_call_target="tpu_custom_call" | custom-call | tf_op jit(solution)/shard_map/pallas_call | solution.py:418

commit v2 on v1

v2 whole, which is shorter than its diff:
```python
import functools

import jax
import jax.numpy as jnp
from jax import lax
from jax.experimental import pallas as pl
from jax.experimental.pallas import tpu as pltpu
from jax.sharding import PartitionSpec as P

STEPS = 6
CENTRE = -205.0 / 72.0
C1, C2, C3, C4 = (8.0 / 5.0, -1.0 / 5.0, 8.0 / 315.0, -1.0 / 560.0)
SCALE = 5040.0
WEIGHTS = tuple(round(SCALE * c) * 1.0 for c in (C1, C2, C3, C4))
W = 4
T = 8
LANES = 128
MESH = pl.DeviceIdType.MESH
def kernel(sizes, now_hbm, before_hbm, code_hbm, vel_hbm, wave_hbm, src_hbm, out_ref, prev_ref,
           field0, field1, beside0, beside1, pack0, pack1, halo, rate, coef, code, source, edge,
           along, along_z, from_edge, only, vel_ref, wave_ref, src_ref, send_sem, recv_sem, load_sem):
    field, beside, pack = (field0, field1), (beside0, beside1), (pack0, pack1)
    (nx, ny, nz), (gx, gy, gz) = sizes
    grid_y, grid_z = ny * gy, nz * gz
    tiles = ny // 8
    fits = LANES // 8
    ix, iy, iz = lax.axis_index("gx"), lax.axis_index("gy"), lax.axis_index("gz")
    targets = (
        (({"gx": lax.rem(ix + gx - 1, gx)}, None), ({"gx": lax.rem(ix + 1, gx)}, None)),
        (({"gy": iy - 1}, iy > 0), ({"gy": iy + 1}, iy < gy - 1)),
        (({"gz": iz - 1}, iz > 0), ({"gz": iz + 1}, iz < gz - 1)),
    )

    def guarded(condition, action):
        if condition is None:
            action()
        else:
            pl.when(condition)(action)

    own_x, own_y = pl.ds(0, nx), pl.ds(T, ny)
    loads = [
        pltpu.make_async_copy(now_hbm, field[0].at[own_x, own_y], load_sem.at[0]),
        pltpu.make_async_copy(before_hbm, field[1].at[own_x, own_y], load_sem.at[1]),
        pltpu.make_async_copy(code_hbm, code, load_sem.at[2]),
        pltpu.make_async_copy(vel_hbm, vel_ref, load_sem.at[3]),
        pltpu.make_async_copy(wave_hbm, wave_ref, load_sem.at[4]),
        pltpu.make_async_copy(src_hbm, src_ref, load_sem.at[5]),
    ]
    for load in loads:
        load.start()

    for par in range(2):
        for rows in (pl.ds(0, T), pl.ds(T + ny, T)):
            beside[par][own_x, rows, :] = jnp.zeros((nx, T, LANES), jnp.float32)
    edge[...] = jnp.zeros_like(edge)

    barrier = pltpu.get_barrier_semaphore()
    for sides in targets:
        for target, present in sides:
            guarded(present, lambda target=target: pl.semaphore_signal(
                barrier, inc=1, device_id=target, device_id_type=MESH))

    nothing = jnp.zeros((nx, T, LANES), jnp.float32)
    for par in range(2):
        field[par][own_x, 0:T, :] = nothing
        field[par][own_x, pl.ds(T + ny, T), :] = nothing
        for inside in (pl.ds(T, T), pl.ds(ny, T)):
            beside[par][own_x, inside, :] = nothing

    faces = list(range(W)) + list(range(nx - W, nx))
    outer, middle = [0, tiles - 1], list(range(1, tiles - 1))
    items = [[(x, g) for x in faces for g in outer], [(x, g) for x in faces for g in middle]]
    rest = [(x, g) for x in range(W, nx - W) for g in range(tiles)]
    items += [rest[n:n + fits] for n in range(0, len(rest), fits)]
    last_slots = list(range(2, len(items)))
    spans = {"low": pl.ds(0, W), "high": pl.ds(nx - W, W), "rest": pl.ds(W, nx - 2 * W)}
    slots = {"outer": pl.ds(0, 1), "middle": pl.ds(1, 1), "rest": pl.ds(2, len(last_slots))}
    bands = {"first": (0, 1), "end": (tiles - 1, 1), "middle": (1, tiles - 2)}

    every = [("x", band, way) for band in bands for way in range(2)]
    every += [("y", part, way) for part in spans for way in range(2)]
    every += [("z", part, way) for part in slots for way in range(2)]
    x_outer = [("x", band, way) for band in ("first", "end") for way in range(2)]
    x_middle = [("x", "middle", way) for way in range(2)]
    y_outer = [("y", part, way) for way in range(2) for part in ("low", "high")]
    y_rest = [("y", "rest", way) for way in range(2)]
    z_of = {part: [("z", part, way) for way in range(2)] for part in slots}

    def transfer(name, par):
        axis, part, way = name
        if axis == "x":
            at, size = bands[part]
            layer = pl.ds(0, W) if way == 0 else pl.ds(nx - W, W)
            src = field[par].at[layer, pl.ds(T + 8 * at, 8 * size)]
            dst = halo.at[par, 1 - way, pl.ds(0, W), pl.ds(8 * at, 8 * size)]
        elif axis == "y":
            own, there = (pl.ds(T, W), pl.ds(T + ny, W)) if way == 0 else (pl.ds(T + ny - W, W), pl.ds(T - W, W))
            src, dst = field[par].at[spans[part], own], beside[par].at[spans[part], there]
        else:
            src, dst = pack[par].at[slots[part]], edge.at[par, 1 - way, slots[part]]
        sides = targets["xyz".index(axis)]
        number = every.index(name)
        copy = pltpu.make_async_remote_copy(
            src_ref=src, dst_ref=dst, send_sem=send_sem.at[par, number], recv_sem=recv_sem.at[par, number],
            device_id=sides[way][0], device_id_type=MESH)
        return copy, sides[way][1], sides[1 - way][1]

    def together(par, names, pick, action):
        groups = []
        for name in names:
            found = transfer(name, par)
            condition = found[pick]
            if groups and groups[-1][0] is condition:
                groups[-1][1].append(found[0])
            else:
                groups.append((condition, [found[0]]))
        for condition, copies in groups:
            guarded(condition, lambda copies=copies: [getattr(copy, action)() for copy in copies] and None)

    def start(par, names):
        together(par, names, 1, "start")

    def wait_sends(par):
        order = sorted(every, key=lambda name: (name[0], name[2]))
        together(par, order, 1, "wait_send")

    def wait_recv(par, names):
        together(par, names, 2, "wait_recv")

    lane = lax.broadcasted_iota(jnp.int32, (8, LANES), 1)
    group_of, place = lane // 8, lane % 8
    zero = jnp.zeros((8, LANES), jnp.float32)

    def packed(value, g, total):
        return jnp.where(group_of == g, pltpu.roll(value, (W + 8 * g) % LANES, 1), total)

    def tile(ref, x, g, shift=0):
        return ref[x, pl.ds(T + 8 * g + shift, 8), :]

    def pack_up(slot):
        total = zero
        for n, (x, g) in enumerate(items[slot]):
            total = packed(tile(field[0], x, g), n, total)
        pack[0][slot] = total

    loads[0].wait()
    for slot in range(2):
        pack_up(slot)
    peers = 2
    for sides in targets[1:]:
        for _, present in sides:
            peers = peers + present.astype(jnp.int32)
    pl.semaphore_wait(barrier, peers)
    start(0, x_outer + z_of["outer"] + y_outer + x_middle + z_of["middle"] + y_rest)
    for slot in last_slots:
        pack_up(slot)
    start(0, z_of["rest"])

    for load in loads[2:]:
        load.wait()
    squares = [vel_ref[n] * vel_ref[n] for n in range(vel_ref.shape[0])]

    def rate_slab(x, carry):
        codes = code[x]
        value = jnp.full(codes.shape, squares[0], jnp.float32)
        for n in range(1, len(squares)):
            value = jnp.where(codes == n, squares[n], value)
        rate[x] = value * (1.0 / SCALE)
        coef[x] = 2.0 + (3.0 * CENTRE) * value
        return carry

    lax.fori_loop(0, nx, rate_slab, 0)

    count = src_ref.shape[0]
    row_at = jnp.full((1, LANES), -1, jnp.int32)
    lane_row = lax.broadcasted_iota(jnp.int32, (1, LANES), 1)
    slot_col = lax.broadcasted_iota(jnp.int32, (LANES, LANES), 0)
    z_at = jnp.full((LANES, LANES), -1, jnp.int32)
    for s in range(count):
        cell = src_ref[s]
        sx = cell // (grid_y * grid_z) - ix * nx
        sy = cell // grid_z % grid_y - iy * ny
        sz = cell % grid_z - iz * nz
        here = (sx >= 0) & (sx < nx) & (sy >= 0) & (sy < ny)
        local = jnp.where(here, sx * ny + sy, -1)
        row_at = jnp.where((lane_row % count == s) & (lane_row < 3 * count), local, row_at)
        z_at = jnp.where((slot_col % count == s) & (slot_col < 3 * count), sz, z_at)
    spread = (z_at == lax.broadcasted_iota(jnp.int32, (LANES, LANES), 1)).astype(jnp.float32).astype(jnp.bfloat16)

    def source_field(t):
        wave = jnp.zeros((1, LANES), jnp.float32)
        for s in range(count):
            wave = jnp.where(lane_row % count == s, wave_ref[t, s], wave)
        high = wave.astype(jnp.bfloat16).astype(jnp.float32)
        rest = wave - high
        middle = rest.astype(jnp.bfloat16).astype(jnp.float32)
        parts = jnp.where(lane_row < count, high, jnp.where(lane_row < 2 * count, middle, rest - middle))
        slabs = LANES // ny

        def chunk(m, carry):
            row = lax.broadcasted_iota(jnp.int32, (LANES, LANES), 0) + m * LANES
            picks = jnp.where(row == row_at, parts, 0.0).astype(jnp.bfloat16)
            value = jnp.dot(picks, spread, preferred_element_type=jnp.float32)
            source[pl.ds(m * slabs, slabs)] = value.reshape(slabs, ny, LANES)
            return carry

        lax.fori_loop(0, nx // slabs, chunk, 0)

    row_in = lax.broadcasted_iota(jnp.int32, (LANES, LANES), 0)
    col_in = lax.broadcasted_iota(jnp.int32, (LANES, LANES), 1)
    spot = row_in % 8
    halo_at = jnp.where(spot < W, spot - W, LANES + spot - W)

    def taps(distance):
        value = jnp.zeros((LANES, LANES), jnp.float32)
        for k in range(1, W + 1):
            value = jnp.where((distance == k) | (distance == -k), WEIGHTS[k - 1], value)
        return value.astype(jnp.bfloat16)

    for part in range(2):
        along_z[pl.ds(part * LANES, LANES), :] = taps(row_in - col_in)
        from_edge[pl.ds(part * LANES, LANES), :] = taps(halo_at - col_in)
    double_lane = lax.broadcasted_iota(jnp.int32, (16, LANES), 1) // 8
    double_row = lax.broadcasted_iota(jnp.int32, (16, LANES), 0) // 8
    for pair in range(8):
        only[pair] = (double_lane == 2 * pair + double_row).astype(jnp.float32).astype(jnp.bfloat16)

    def split(value):
        high = value.astype(jnp.bfloat16)
        return high, (value - high.astype(jnp.float32)).astype(jnp.bfloat16)

    def z_own(cur):
        value = field[cur][own_x, own_y, :].reshape(nx * ny, LANES)
        total = jnp.dot(jnp.concatenate(split(value), axis=1), along_z[...], preferred_element_type=jnp.float32)
        along[...] = total.reshape(nx, ny, LANES)

    def z_beside(cur, chosen):
        picked = []
        for slot in chosen:
            value = jnp.where(place < W, edge[cur, 0, slot], edge[cur, 1, slot])
            high, low = split(jnp.concatenate([value, value], axis=0))
            picked += [jnp.concatenate([high * only[pair], low * only[pair]], axis=1) for pair in range(8)]
        total = jnp.dot(jnp.concatenate(picked, axis=0), from_edge[...], preferred_element_type=jnp.float32)
        return total.reshape(len(chosen), fits, 8, LANES)

    def own_part(cur, nxt):
        for x in range(nx):
            for g in range(tiles):
                at = pl.ds(8 * g, 8)
                acc = along[x, at, :]
                for k in range(1, W + 1):
                    near = tile(field[cur], x, g, k) + tile(field[cur], x, g, -k)
                    if x + k < nx:
                        near = near + tile(field[cur], x + k, g)
                    if x - k >= 0:
                        near = near + tile(field[cur], x - k, g)
                    acc = acc + WEIGHTS[k - 1] * near
                start_at = coef[x, at, :] * tile(field[cur], x, g) - tile(field[nxt], x, g)
                field[nxt][x, pl.ds(T + 8 * g, 8), :] = start_at + (rate[x, at, :] * acc + source[x, at, :])

    def y_part(cur, x, g):
        acc = None
        for k in range(1, W + 1):
            for edge_tile, shift in ((0, -k), (tiles - 1, k)):
                if g == edge_tile:
                    term = WEIGHTS[k - 1] * tile(beside[cur], x, g, shift)
                    acc = term if acc is None else acc + term
        return acc

    def x_part(cur, x, g):
        acc, at = None, pl.ds(8 * g, 8)
        for k in range(1, W + 1):
            if x - k < 0:
                term = WEIGHTS[k - 1] * halo[cur, 0, x - k + W, at, :]
            elif x + k >= nx:
                term = WEIGHTS[k - 1] * halo[cur, 1, x + k - nx, at, :]
            else:
                continue
            acc = term if acc is None else acc + term
        return acc

    loads[1].wait()
    for t in range(STEPS):
        cur, nxt = t % 2, (t + 1) % 2
        last = t == STEPS - 1

        def put(x, g, value):
            own = pl.ds(8 * g, 8)
            if last:
                out_ref[x, own, :] = value
            else:
                field[nxt][x, pl.ds(T + 8 * g, 8), :] = value
            if t == STEPS - 2:
                prev_ref[x, own, :] = value

        source_field(t)
        if t >= 1:
            wait_sends(nxt)
        z_own(cur)
        own_part(cur, nxt)
        for slot, part in enumerate(("outer", "middle")):
            wait_recv(cur, z_of[part])
            beyond = z_beside(cur, [slot])[0]
            if slot == 0:
                wait_recv(cur, y_outer)
            so_far = []
            for n, (x, g) in enumerate(items[slot]):
                acc, more = beyond[n], y_part(cur, x, g)
                so_far.append(tile(field[nxt], x, g) + rate[x, pl.ds(8 * g, 8), :] * (acc if more is None else acc + more))
            xs = x_outer if slot == 0 else x_middle
            wait_recv(cur, xs)
            total = zero
            for n, (x, g) in enumerate(items[slot]):
                value = so_far[n] + rate[x, pl.ds(8 * g, 8), :] * x_part(cur, x, g)
                put(x, g, value)
                if not last:
                    total = packed(value, n, total)
            if not last:
                start(nxt, xs)
                pack[nxt][slot] = total
                start(nxt, z_of[part] + (y_outer if slot == 0 else []))
        wait_recv(cur, z_of["rest"])
        beyond = z_beside(cur, last_slots)
        wait_recv(cur, y_rest)
        for m, slot in enumerate(last_slots):
            total = zero
            for n, (x, g) in enumerate(items[slot]):
                acc, more = beyond[m, n], y_part(cur, x, g)
                value = tile(field[nxt], x, g) + rate[x, pl.ds(8 * g, 8), :] * (acc if more is None else acc + more)
                put(x, g, value)
                if not last:
                    total = packed(value, n, total)
            if not last:
                pack[nxt][slot] = total
        if not last:
            start(nxt, z_of["rest"] + y_rest)
    wait_sends((STEPS - 1) % 2)


def move_out(first_ref, second_ref, first_out, second_out, sem):
    moves = [
        pltpu.make_async_copy(first_ref, first_out, sem.at[0]),
        pltpu.make_async_copy(second_ref, second_out, sem.at[1]),
    ]
    for move in moves:
        move.start()
    for move in moves:
        move.wait()


def solution(mesh):
    counts = tuple(mesh.shape[name] for name in ("gx", "gy", "gz"))

    def per_device(now, before, codes, velocity, wavelet, source_cell):
        nx, ny, nz = now.shape
        anywhere = pl.BlockSpec(memory_space=pl.ANY)
        packs = nx * ny // LANES
        copies = 18
        results = pl.pallas_call(
            functools.partial(kernel, (now.shape, counts)),
            out_shape=(pltpu.VMEM(now.shape, jnp.float32),) * 2,
            in_specs=[anywhere] * 6,
            out_specs=(pl.BlockSpec(memory_space=pltpu.VMEM),) * 2,
            scratch_shapes=[
                pltpu.VMEM((nx, ny + 2 * T, nz), jnp.float32),
                pltpu.VMEM((nx, ny + 2 * T, nz), jnp.float32),
                pltpu.VMEM((nx, ny + 2 * T, nz), jnp.float32),
                pltpu.VMEM((nx, ny + 2 * T, nz), jnp.float32),
                pltpu.VMEM((packs, 8, LANES), jnp.float32),
                pltpu.VMEM((packs, 8, LANES), jnp.float32),
                pltpu.VMEM((2, 2, W, ny, nz), jnp.float32),
                pltpu.VMEM((nx, ny, nz), jnp.float32),
                pltpu.VMEM((nx, ny, nz), jnp.float32),
                pltpu.VMEM((nx, ny, nz), jnp.int32),
                pltpu.VMEM((nx, ny, nz), jnp.float32),
                pltpu.VMEM((2, 2, packs, 8, LANES), jnp.float32),
                pltpu.VMEM((nx, ny, nz), jnp.float32),
                pltpu.VMEM((2 * LANES, LANES), jnp.bfloat16),
                pltpu.VMEM((2 * LANES, LANES), jnp.bfloat16),
                pltpu.VMEM((8, 16, LANES), jnp.bfloat16),
                pltpu.SMEM(velocity.shape, jnp.float32),
                pltpu.SMEM(wavelet.shape, jnp.float32),
                pltpu.SMEM(source_cell.shape, jnp.int32),
                pltpu.SemaphoreType.DMA((2, copies)),
                pltpu.SemaphoreType.DMA((2, copies)),
                pltpu.SemaphoreType.DMA((6,)),
            ],
            compiler_params=pltpu.CompilerParams(collective_id=0, has_side_effects=True),
        )(now, before, codes, velocity, wavelet, source_cell)
        return pl.pallas_call(
            move_out,
            out_shape=(jax.ShapeDtypeStruct(now.shape, jnp.float32),) * 2,
            in_specs=[pl.BlockSpec(memory_space=pltpu.VMEM)] * 2,
            out_specs=(anywhere, anywhere),
            scratch_shapes=[pltpu.SemaphoreType.DMA((2,))],
            compiler_params=pltpu.CompilerParams(vmem_limit_bytes=2**20),
        )(*[pltpu.with_memory_space_constraint(value, pltpu.VMEM) for value in results])

    block = P("gx", "gy", "gz")
    return jax.shard_map(
        per_device,
        mesh=mesh,
        in_specs=(block, block, block, P(), P(), P()),
        out_specs=(block, block),
        check_vma=False,
    )
```

time: 26.8 us -> 25.4 us (0.948)
  Pallas kernels: 25.9 us -> 24.6 us
    pallas_call x1, Pallas kernels: 25.1 us -> 23.8 us  [per_device(): pl.pallas_call(functools.partial(kernel, (now.shape, counts)), out_shape=...]
where the time goes in v2:
time: 25.4 us; the launch traced here: 25.3 us
  Pallas kernels  24.6 us (97%)
  between operations  0.64 us (3%)
    pallas_call x1, Pallas kernels, per_device(): pl.pallas_call(functools.partial(kernel, (now.shape, counts)), out_shape=...  23.8 us
    pallas_call x1, Pallas kernels, per_device(): pl.pallas_call(move_out, out_shape=(jax.ShapeDtypeStruct(now.shape, jnp.f...  0.81 us

profile of v2, /device:TPU:0, one launch (start us, length us, event | category | flops | bytes accessed | tf_op | source)
XLA Modules:
  0.0 25.3 jit_solution(13210992258715964854)
XLA Ops:
  0.6 23.8 %shard_map.77 = (f32[16,32,128]{2,1,0:T(8,128)S(1)}, f32[16,32,128]{2,1,0:T(8,128)S(1)}) custom-call(f32[16,32,128]{2,1,0:T(8,128)} %now_hbm.1, f32[16,32,128]{2,1,0:T(8,128)} %before_hbm.1, s32[16,32,128]{2,1,0:T(8,128)} %code_hbm.1, f32[8]{0:T(128)} %vel_hbm.1, f32[6,16]{1,0:T(8,128)} %wave_hbm.1, s32[16]{0:T(128)} %src_hbm.1), custom_call_target="tpu_custom_call" | custom-call | tf_op jit(solution)/shard_map/pallas_call | solution.py:359
  24.5 0.8 %shard_map.78 = (f32[16,32,128]{2,1,0:T(8,128)}, f32[16,32,128]{2,1,0:T(8,128)}) custom-call(f32[16,32,128]{2,1,0:T(8,128)S(1)} %get-tuple-element.4.first_ref, f32[16,32,128]{2,1,0:T(8,128)S(1)} %get-tuple-element.5.second_ref), custom_call_target="tpu_custom_call" | custom-call | tf_op jit(solution)/shard_map/pallas_call | solution.py:390

commit v3 on v2

--- a/solution.py
+++ b/solution.py
@@ -337,6 +337,16 @@
     wait_sends((STEPS - 1) % 2)
 
 
+def scoped(sizes, *refs):
+    copies = 18
+    pl.run_scoped(
+        functools.partial(kernel, sizes, *refs),
+        pltpu.SemaphoreType.DMA((2, copies)),
+        pltpu.SemaphoreType.DMA((2, copies)),
+        pltpu.SemaphoreType.DMA((6,)),
+    )
+
+
 def move_out(first_ref, second_ref, first_out, second_out, sem):
     moves = [
         pltpu.make_async_copy(first_ref, first_out, sem.at[0]),
@@ -355,9 +365,8 @@
         nx, ny, nz = now.shape
         anywhere = pl.BlockSpec(memory_space=pl.ANY)
         packs = nx * ny // LANES
-        copies = 18
         results = pl.pallas_call(
-            functools.partial(kernel, (now.shape, counts)),
+            functools.partial(scoped, (now.shape, counts)),
             out_shape=(pltpu.VMEM(now.shape, jnp.float32),) * 2,
             in_specs=[anywhere] * 6,
             out_specs=(pl.BlockSpec(memory_space=pltpu.VMEM),) * 2,
@@ -381,9 +390,6 @@
                 pltpu.SMEM(velocity.shape, jnp.float32),
                 pltpu.SMEM(wavelet.shape, jnp.float32),
                 pltpu.SMEM(source_cell.shape, jnp.int32),
-                pltpu.SemaphoreType.DMA((2, copies)),
-                pltpu.SemaphoreType.DMA((2, copies)),
-                pltpu.SemaphoreType.DMA((6,)),
             ],
             compiler_params=pltpu.CompilerParams(collective_id=0, has_side_effects=True),
         )(now, before, codes, velocity, wavelet, source_cell)

time: 25.4 us -> 24.7 us (0.972)
  Pallas kernels: 24.6 us -> 23.9 us
    pallas_call x1, Pallas kernels: 23.8 us -> 23.1 us  [per_device(): pl.pallas_call(functools.partial(scoped, (now.shape, counts)), out_shape=...]
where the time goes in v3:
time: 24.7 us; the launch traced here: 24.6 us
  Pallas kernels  23.9 us (97%)
  between operations  0.64 us (3%)
    pallas_call x1, Pallas kernels, per_device(): pl.pallas_call(functools.partial(scoped, (now.shape, counts)), out_shape=...  23.1 us
    pallas_call x1, Pallas kernels, per_device(): pl.pallas_call(move_out, out_shape=(jax.ShapeDtypeStruct(now.shape, jnp.f...  0.81 us

profile of v3, /device:TPU:0, one launch (start us, length us, event | category | flops | bytes accessed | tf_op | source)
XLA Modules:
  0.0 24.6 jit_solution(15331232276881851494)
XLA Ops:
  0.6 23.1 %shard_map.77 = (f32[16,32,128]{2,1,0:T(8,128)S(1)}, f32[16,32,128]{2,1,0:T(8,128)S(1)}) custom-call(f32[16,32,128]{2,1,0:T(8,128)} %refs_0_.1, f32[16,32,128]{2,1,0:T(8,128)} %refs_1_.1, s32[16,32,128]{2,1,0:T(8,128)} %refs_2_.1, f32[8]{0:T(128)} %refs_3_.1, f32[6,16]{1,0:T(8,128)} %refs_4_.1, s32[16]{0:T(128)} %refs_5_.1), custom_call_target="tpu_custom_call" | custom-call | tf_op jit(solution)/shard_map/pallas_call | solution.py:368
  23.8 0.8 %shard_map.78 = (f32[16,32,128]{2,1,0:T(8,128)}, f32[16,32,128]{2,1,0:T(8,128)}) custom-call(f32[16,32,128]{2,1,0:T(8,128)S(1)} %get-tuple-element.4.first_ref, f32[16,32,128]{2,1,0:T(8,128)S(1)} %get-tuple-element.5.second_ref), custom_call_target="tpu_custom_call" | custom-call | tf_op jit(solution)/shard_map/pallas_call | solution.py:396

commit v4 on v3

--- a/solution.py
+++ b/solution.py
@@ -49,11 +49,6 @@
     for load in loads:
         load.start()
 
-    for par in range(2):
-        for rows in (pl.ds(0, T), pl.ds(T + ny, T)):
-            beside[par][own_x, rows, :] = jnp.zeros((nx, T, LANES), jnp.float32)
-    edge[...] = jnp.zeros_like(edge)
-
     barrier = pltpu.get_barrier_semaphore()
     for sides in targets:
         for target, present in sides:
@@ -61,6 +56,21 @@
                 barrier, inc=1, device_id=target, device_id_type=MESH))
 
     nothing = jnp.zeros((nx, T, LANES), jnp.float32)
+
+    def clear(way):
+        def rows():
+            for par in range(2):
+                beside[par][own_x, pl.ds(way * (T + ny), T), :] = nothing
+
+        def packs():
+            for par in range(2):
+                edge[par, way] = jnp.zeros(edge.shape[2:], jnp.float32)
+
+        pl.when(jnp.logical_not(targets[1][way][1]))(rows)
+        pl.when(jnp.logical_not(targets[2][way][1]))(packs)
+
+    clear(0)
+    clear(1)
     for par in range(2):
         field[par][own_x, 0:T, :] = nothing
         field[par][own_x, pl.ds(T + ny, T), :] = nothing
@@ -144,14 +154,16 @@
         pack[0][slot] = total
 
     loads[0].wait()
-    for slot in range(2):
-        pack_up(slot)
     peers = 2
     for sides in targets[1:]:
         for _, present in sides:
             peers = peers + present.astype(jnp.int32)
     pl.semaphore_wait(barrier, peers)
-    start(0, x_outer + z_of["outer"] + y_outer + x_middle + z_of["middle"] + y_rest)
+    start(0, x_outer)
+    pack_up(0)
+    start(0, z_of["outer"] + y_outer + x_middle)
+    pack_up(1)
+    start(0, z_of["middle"] + y_rest)
     for slot in last_slots:
         pack_up(slot)
     start(0, z_of["rest"])
@@ -239,9 +251,10 @@
         for slot in chosen:
             value = jnp.where(place < W, edge[cur, 0, slot], edge[cur, 1, slot])
             high, low = split(jnp.concatenate([value, value], axis=0))
-            picked += [jnp.concatenate([high * only[pair], low * only[pair]], axis=1) for pair in range(8)]
-        total = jnp.dot(jnp.concatenate(picked, axis=0), from_edge[...], preferred_element_type=jnp.float32)
-        return total.reshape(len(chosen), fits, 8, LANES)
+            picked += [high * only[pair] for pair in range(8)] + [low * only[pair] for pair in range(8)]
+        total = jnp.dot(jnp.concatenate(picked, axis=0), from_edge[0:LANES, :], preferred_element_type=jnp.float32)
+        total = total.reshape(len(chosen), 2, fits, 8, LANES)
+        return total[:, 0] + total[:, 1]
 
     def own_part(cur, nxt):
         for x in range(nx):

time: 24.7 us -> 24.8 us (level)
  no operation moved by 1% of the time
where the time goes in v4:
time: 24.8 us; the launch traced here: 24.6 us
  Pallas kernels  24 us (97%)
  between operations  0.64 us (3%)
    pallas_call x1, Pallas kernels, per_device(): pl.pallas_call(functools.partial(scoped, (now.shape, counts)), out_shape=...  23.2 us
    pallas_call x1, Pallas kernels, per_device(): pl.pallas_call(move_out, out_shape=(jax.ShapeDtypeStruct(now.shape, jnp.f...  0.81 us

profile of v4, /device:TPU:0, one launch (start us, length us, event | category | flops | bytes accessed | tf_op | source)
XLA Modules:
  0.0 24.6 jit_solution(16830440766379634163)
XLA Ops:
  0.6 23.2 %shard_map.77 = (f32[16,32,128]{2,1,0:T(8,128)S(1)}, f32[16,32,128]{2,1,0:T(8,128)S(1)}) custom-call(f32[16,32,128]{2,1,0:T(8,128)} %refs_0_.1, f32[16,32,128]{2,1,0:T(8,128)} %refs_1_.1, s32[16,32,128]{2,1,0:T(8,128)} %refs_2_.1, f32[8]{0:T(128)} %refs_3_.1, f32[6,16]{1,0:T(8,128)} %refs_4_.1, s32[16]{0:T(128)} %refs_5_.1), custom_call_target="tpu_custom_call" | custom-call | tf_op jit(solution)/shard_map/pallas_call | solution.py:381
  23.8 0.8 %shard_map.78 = (f32[16,32,128]{2,1,0:T(8,128)}, f32[16,32,128]{2,1,0:T(8,128)}) custom-call(f32[16,32,128]{2,1,0:T(8,128)S(1)} %get-tuple-element.4.first_ref, f32[16,32,128]{2,1,0:T(8,128)S(1)} %get-tuple-element.5.second_ref), custom_call_target="tpu_custom_call" | custom-call | tf_op jit(solution)/shard_map/pallas_call | solution.py:409
